TPU v7x, 256 devices: a whole 4x4x8 slice. The times are simulated.
256 devices in a mesh: tp: 4 (over x), dp: 64 (over z, y, core).
Axes of the slice: x: 4, y: 4, z: 8, core: 2. Of those that a mesh axis runs over, the one named last changes fastest.
Arguments:
- item_query: bfloat16 [8192, 2048], P('dp', 'tp'), may hold values from -20 to 20, as said below
- item_keys: bfloat16 [8192, 4, 2048], P('dp', None, 'tp'), may hold values from -20 to 20
- item_values: bfloat16 [8192, 4, 2048], P('dp', None, 'tp'), may hold values from -6 to 6
- item_out_weight: bfloat16 [2048, 4096], P('tp'), may hold values from -0.125 to 0.125
- item_residual: bfloat16 [8192, 4096], P('dp'), may hold values from -3 to 3
- cite_home: int32 [65536, 1], P('dp'), may hold values from 0 to 63; in each aligned block of 1024 rows (0 to 1023, 1024 to 2047, ...) at most 24 rows name the same one
- cite_row: int32 [65536], P('dp'), may hold values from 0 to 127
- seq_length: int32 [64], P('dp'), may hold values from 1 to 1024, 40960 in all
- user_gain: float32 [4096], replicated, may hold values from 0.1 to 1.9
- user_weight: bfloat16 [4096, 16, 384], P('dp', 'tp'), may hold values from -0.09375 to 0.09375
Outputs:
- user_qkv: bfloat16 [65536, 16, 384], P('dp', 'tp')
Inputs may be any that keep to these rules, and one draw needn't show every extreme that they name: `item_query`: in hidden draws some items' queries equal a multiple of keys at their last two tokens. `cite_home`: among the 1024 positions of one sequence at most 24 cite items of one home device, and some home device is cited exactly 24 times. `seq_length`: some sequence has all 1024 positions live.
All inputs are finite; a program needn't handle non-finite values. No bound on the sum of `seq_length` on one device may be relied on, other than what follows from the above.
Results may differ from a plain program's by a relative error of at most 0.0065.
Values may be sent and summed in bfloat16 or wider, within the bound.
No kernel may reach another device: no remote copies, remote signals or barrier semaphores. Data moves between devices by JAX's collectives and lax.ppermute only.
A program may use at most 128 MiB of HBM per device.

v0:
```python
import math
import jax
import jax.numpy as jnp
from jax import lax
from jax.sharding import PartitionSpec as P

HEAD_DIM = 128


def cut_along(x, dim, size):
    before, after = (x.shape[:dim], x.shape[dim + 1 :])
    return jnp.moveaxis(x.reshape(*before, size, -1, *after), dim, 0)


def sent_and_summed(x, axis, dim):
    parts = cut_along(x, dim, lax.axis_size(axis))
    arrived = lax.all_to_all(parts, axis, split_axis=0, concat_axis=0, tiled=True)
    return arrived.sum(axis=0)


def per_device(
    item_query,
    item_keys,
    item_values,
    item_out_weight,
    item_residual,
    cite_home,
    cite_row,
    seq_length,
    user_gain,
    user_weight,
):
    count_items, width_heads = item_query.shape
    tokens_item = item_keys.shape[1]
    local_heads = width_heads // HEAD_DIM
    queries = item_query.reshape(count_items, local_heads, HEAD_DIM)
    keys_all = item_keys.reshape(count_items, tokens_item, local_heads, HEAD_DIM)
    values_all = item_values.reshape(count_items, tokens_item, local_heads, HEAD_DIM)
    scores = jnp.einsum("ihd,ithd->iht", queries, keys_all, preferred_element_type=jnp.float32) * (
        1.0 / math.sqrt(HEAD_DIM)
    )
    probs = jax.nn.softmax(scores, axis=-1).astype(jnp.bfloat16)
    attended = jnp.einsum("iht,ithd->ihd", probs, values_all, preferred_element_type=jnp.float32)
    attended = attended.astype(jnp.bfloat16).reshape(count_items, width_heads)
    partial_value = jnp.dot(attended, item_out_weight, preferred_element_type=jnp.float32)
    summed = sent_and_summed(partial_value, "tp", 1)
    columns = summed.shape[1]
    own_cols = lax.dynamic_slice_in_dim(item_residual, lax.axis_index("tp") * columns, columns, 1)
    item_vec = (summed + own_cols.astype(jnp.float32)).astype(jnp.bfloat16)
    home_dev = cite_home[:, 0]
    length_seq = home_dev.shape[0]
    devices = lax.axis_size("dp")
    capacity = 3 * length_seq // (2 * devices)
    onehot = (home_dev[:, None] == jnp.arange(devices, dtype=jnp.int32)[None, :]).astype(jnp.int32)
    before = jnp.cumsum(onehot, axis=0) - onehot
    slot_index = jnp.sum(before * onehot, axis=1)
    target = home_dev * capacity + slot_index
    wanted = (
        jnp.zeros((devices * capacity,), jnp.int32)
        .at[target]
        .set(cite_row)
        .reshape(devices, capacity)
    )
    asked = lax.all_to_all(wanted, "dp", split_axis=0, concat_axis=0, tiled=True)
    looked = jnp.take(item_vec, asked.reshape(-1), axis=0).reshape(
        devices, capacity, item_vec.shape[1]
    )
    answers = lax.all_to_all(looked, "dp", split_axis=0, concat_axis=0, tiled=True)
    cited = jnp.take(answers.reshape(devices * capacity, item_vec.shape[1]), target, axis=0)
    cited = lax.all_gather(cited, "tp", axis=1, tiled=True)
    values32 = cited.astype(jnp.float32)
    scale = lax.rsqrt(jnp.mean(values32 * values32, axis=1, keepdims=True) + 1e-05)
    normed = (values32 * scale * user_gain[None, :]).astype(jnp.bfloat16)
    shard_rows, user_heads, triple = user_weight.shape
    weight_flat = user_weight.reshape(shard_rows, user_heads * triple)
    projected = jnp.dot(
        normed,
        lax.all_gather(weight_flat, "dp", axis=0, tiled=True),
        preferred_element_type=jnp.float32,
    )
    live = jnp.arange(length_seq, dtype=jnp.int32) < seq_length[0]
    masked = jnp.where(live[:, None], projected, jnp.zeros_like(projected))
    return masked.astype(jnp.bfloat16).reshape(length_seq, user_heads, triple)


def solution(mesh):
    in_specs = (
        P("dp", "tp"),
        P("dp", None, "tp"),
        P("dp", None, "tp"),
        P("tp", None),
        P("dp", None),
        P("dp", None),
        P("dp"),
        P("dp"),
        P(),
        P("dp", "tp", None),
    )
    out_specs = P("dp", "tp", None)
    return jax.shard_map(
        per_device, mesh=mesh, in_specs=in_specs, out_specs=out_specs, check_vma=False
    )
```

profile of v0, /device:TPU:1, one launch (start us, length us, event | category | flops | bytes accessed | tf_op | source)
XLA Modules:
  0.0 401.7 jit_solution(5603883770292417331)
XLA Ops:
  6.5 0.8 fusion.23
  7.3 18.0 %reduce-window.6 = s32[64,8,128]{2,1,0:T(8,128)S(1)} reduce-window(s32[64,8,128]{2,1,0:T(8,128)S(1)} %fusion.23, s32[]{:T(128)} %constant.20.clone.1), window={size=1x1x128 pad=0_0x0_0x127_0}, to_apply=%region_0.0 | reduce-window | flops 8323072 | bytes 524292 | tf_op jit(solution)/shard_map/reduce-window
  25.9 0.8 fusion.22
  26.6 0.7 and_reduce_fusion
  27.4 4.5 %scatter_custom_fusion = s32[1536]{0:T(1024)S(1)} fusion(s32[1024]{0:T(1024)S(1)} %bitcast.69, s32[1024]{0:T(1024)} %param.16, s32[]{:T(128)} %constant.20.clone.1), kind=kCustom, calls=%fused_computation.46 | custom fusion | bytes 6656 | tf_op jit(solution)/shard_map/scatter | solution.py:61
  31.8 0.7 all_to_all.12
  32.5 13.1 %all-to-all-start = ((s32[64,1,24]{2,1,0:T(1,128)}), s32[64,1,24]{2,1,0:T(1,128)S(1)}, u32[]{:S(2)}, u32[]{:S(2)}) async-start(s32[64,1,24]{2,1,0:T(1,128)} %bitcast.7), calls=%async_computation | async-start | bytes 65536 | tf_op jit(solution)/shard_map/all_to_all | solution.py:64
  45.7 1.3 reshape.152
  47.0 1.7 fusion.18
  48.9 0.2 copy.26
  49.1 0.7 fusion.16
  49.9 6.5 %copy.29 = bf16[4096,512]{1,0:T(8,128)(2,1)} copy(bf16[4096,512]{0,1:T(8,128)(2,1)} %bitcast.59) | data formatting | bytes 8388608 | tf_op jit(solution)/shard_map/dot_general | solution.py:45
  56.4 5.0 %convolution_bitcast_fusion = f32[4,128,1024]{2,1,0:T(8,128)} fusion(bf16[128,512,1]{1,0,2:T(8,128)(2,1)S(1)} %reshape.150, bf16[4,1024,512]{2,1,0:T(8,128)(2,1)} %bitcast.57), kind=kOutput, calls=%fused_computation.16 | convolution fusion | flops 536870912 | bytes 6422528 | tf_op jit(solution)/shard_map/dot_general | solution.py:45
  61.3 4.0 %all-to-all-start.1 = ((f32[4,128,1024]{2,1,0:T(8,128)}), f32[4,128,1024]{2,1,0:T(8,128)S(1)}, u32[]{:S(2)}, u32[]{:S(2)}) async-start(f32[4,128,1024]{2,1,0:T(8,128)} %convolution_bitcast_fusion), calls=%async_computation.1 | async-start | bytes 4194304 | tf_op jit(solution)/shard_map/all_to_all | solution.py:17
  65.4 0.6 broadcast.90
  66.0 0.8 reduce.7
  66.9 24.2 %all-to-all-done.1 = f32[4,128,1024]{2,1,0:T(8,128)S(1)} async-done(((f32[4,128,1024]{2,1,0:T(8,128)}), f32[4,128,1024]{2,1,0:T(8,128)S(1)}, u32[]{:S(2)}, u32[]{:S(2)}) %all-to-all-start.1) | async-done | bytes 2097184 | tf_op jit(solution)/shard_map/all_to_all | solution.py:17
  91.1 0.2 reduce_sum.41
  91.3 1.0 add_convert_fusion
  92.3 5.8 %gather_fusion = bf16[1536,1024]{1,0:T(8,128)(2,1)} fusion(bf16[128,1024]{1,0:T(8,128)(2,1)S(1)} %add_convert_fusion, s32[2048]{0:T(1024)S(1)} %pad_clamp_fusion), kind=kCustom, calls=%fused_computation | custom fusion | bytes 6297600 | tf_op jit(solution)/shard_map/jit(_take)/gather | solution.py:65
  98.1 3.3 broadcast_select_fusion
  101.3 11.7 %all-to-all-start.2 = ((bf16[64,24,1024]{2,1,0:T(8,128)(2,1)}), bf16[64,24,1024]{2,1,0:T(8,128)(2,1)}, u32[]{:S(2)}, u32[]{:S(2)}) async-start(bf16[64,24,1024]{2,1,0:T(8,128)(2,1)} %broadcast_select_fusion), calls=%async_computation.2 | async-start | bytes 6291456 | tf_op jit(solution)/shard_map/all_to_all | solution.py:68
  113.1 72.3 %all-to-all-done.2 = bf16[64,24,1024]{2,1,0:T(8,128)(2,1)} async-done(((bf16[64,24,1024]{2,1,0:T(8,128)(2,1)}), bf16[64,24,1024]{2,1,0:T(8,128)(2,1)}, u32[]{:S(2)}, u32[]{:S(2)}) %all-to-all-start.2) | async-done | bytes 3145760 | tf_op jit(solution)/shard_map/all_to_all | solution.py:68
  185.4 7.3 %gather_fusion.1 = bf16[1024,1024]{1,0:T(8,128)(2,1)S(1)} fusion(bf16[1536,1024]{1,0:T(8,128)(2,1)} %bitcast.19, s32[1024]{0:T(1024)S(1)} %broadcast_clamp_fusion), kind=kCustom, calls=%fused_computation.1 | custom fusion | bytes 4198400 | tf_op jit(solution)/shard_map/jit(_take)/gather | solution.py:69
  192.7 1.6 broadcast_select_fusion.1
  194.3 0.2 all-gather.5.cloned.1.call-start
  194.5 0.7 copy.31
  195.9 79.5 %all-gather.3.cloned.1.call-done = bf16[1024,4096]{1,0:T(8,128)(2,1)} async-done(((bf16[1024,1024]{1,0:T(8,128)(2,1)}), bf16[1024,4096]{1,0:T(8,128)(2,1)}) %all-gather.3.cloned.1.call-update) | async-done | bytes 8388624 | tf_op jit(solution)/shard_map/all_gather | solution.py:70
  275.4 5.1 %fusion.2 = f32[1024]{0:T(1024)S(1)} fusion(bf16[1024,4096]{1,0:T(8,128)(2,1)} %all-gather.3.cloned.1.call-done), kind=kLoop, calls=%fused_computation.7 | loop fusion | flops 12581888 | bytes 8392704 | tf_op jit(solution)/shard_map/reduce_sum | solution.py:72
  280.5 88.8 %all-gather.5.cloned.1.call-done = bf16[4096,1536]{1,0:T(8,128)(2,1)} async-done(((bf16[64,1536]{1,0:T(8,128)(2,1)}), bf16[4096,1536]{1,0:T(8,128)(2,1)}) %all-gather.5.cloned.1.call-update) | async-done | bytes 12582928 | tf_op jit(solution)/shard_map/all_gather | solution.py:78
  369.3 19.3 %select_convert_fusion = bf16[1024,1536]{1,0:T(8,128)(2,1)} fusion(bf16[4096,1536]{1,0:T(8,128)(2,1)} %all-gather.5.cloned.1.call-done, bf16[1024,4096]{1,0:T(8,128)(2,1)} %all-gather.3.cloned.1.call-done, f32[4096]{0:T(1024)S(1)} %copy-done.2, f32[1024]{0:T(1024)S(1)} %add_rsqrt_fusion, pred[1024]{0:T(1024)(128)(4,1)S(1)} %iota_compare_fusion.2), kind=kOutput, calls=%fused_computation.13 | convolution fusion | flops 12904824832 | bytes 24138752 | tf_op jit(solution)/shard_map/dot_general | solution.py:76
  388.6 6.2 %reshape.121 = bf16[1024,4,384]{2,1,0:T(4,128)(2,1)} reshape(bf16[1024,1536]{1,0:T(8,128)(2,1)} %select_convert_fusion) | data formatting | bytes 6291456 | tf_op jit(solution)/shard_map/reshape | solution.py:83
  (27 shorter events, 1.0 us)
Async XLA Ops:
  6.5 42.5 %copy-start = (bf16[128,4,512]{2,1,0:T(4,128)(2,1)S(1)}, bf16[128,4,512]{2,1,0:T(4,128)(2,1)}, u32[]{:S(2)}) copy-start(bf16[128,4,512]{2,1,0:T(4,128)(2,1)} %param.12) | copy-start | bytes 1572868
  32.5 28.8 %all-to-all-start = ((s32[64,1,24]{2,1,0:T(1,128)}), s32[64,1,24]{2,1,0:T(1,128)S(1)}, u32[]{:S(2)}, u32[]{:S(2)}) async-start(s32[64,1,24]{2,1,0:T(1,128)} %bitcast.7), calls=%async_computation | async-start | bytes 65536 | tf_op jit(solution)/shard_map/all_to_all | solution.py:64
  61.3 29.7 %all-to-all-start.1 = ((f32[4,128,1024]{2,1,0:T(8,128)}), f32[4,128,1024]{2,1,0:T(8,128)S(1)}, u32[]{:S(2)}, u32[]{:S(2)}) async-start(f32[4,128,1024]{2,1,0:T(8,128)} %convolution_bitcast_fusion), calls=%async_computation.1 | async-start | bytes 4194304 | tf_op jit(solution)/shard_map/all_to_all | solution.py:17
  101.3 84.0 %all-to-all-start.2 = ((bf16[64,24,1024]{2,1,0:T(8,128)(2,1)}), bf16[64,24,1024]{2,1,0:T(8,128)(2,1)}, u32[]{:S(2)}, u32[]{:S(2)}) async-start(bf16[64,24,1024]{2,1,0:T(8,128)(2,1)} %broadcast_select_fusion), calls=%async_computation.2 | async-start | bytes 6291456 | tf_op jit(solution)/shard_map/all_to_all | solution.py:68
  113.0 162.4 %all-gather.3.cloned.1.call-start = ((), (), s32[]{:S(2)}) async-start(), calls=%async_computation.3 | async-start | bytes 10485760 | tf_op jit(solution)/shard_map/all_gather | solution.py:70
  192.7 1.9 copy-start.1
  194.3 175.0 %all-gather.5.cloned.1.call-start = ((), (), s32[]{:S(2)}) async-start(), calls=%async_computation.4 | async-start | bytes 12779520 | tf_op jit(solution)/shard_map/all_gather | solution.py:78
  195.9 173.3 %copy-start.2 = (f32[4096]{0:T(1024)S(1)}, f32[4096]{0:T(1024)}, u32[]{:S(2)}) copy-start(f32[4096]{0:T(1024)} %param.18) | copy-start | bytes 49156
Sparse Core Ops, SparseCore 0:
  194.4 80.9 all-gather.2
  278.1 91.0 all-gather.4
where the time goes:
time: 403 us; the launch traced here: 402 us
  waiting for transfers between devices  265 us (66%)
  local copies, waits for them, and re-layouts  34.3 us (9%)
  other arithmetic  32.5 us (8%)
  starting transfers between devices  29.1 us (7%)
  matrix products  26.7 us (7%)
  between operations  14.3 us (4%)
    all_gather x1, waiting for transfers between devices, per_device(): lax.all_gather(weight_flat, 'dp', axis=0, tiled=True)  88.8 us
    all_gather x1, waiting for transfers between devices, per_device(): cited = lax.all_gather(cited, 'tp', axis=1, tiled=True)  79.5 us
    all_to_all x1, waiting for transfers between devices, per_device(): lax.all_to_all(looked, 'dp', split_axis=0, concat_axis=0, tiled=True)  72.3 us
    all_to_all x1, waiting for transfers between devices, sent_and_summed(): lax.all_to_all(parts, axis, split_axis=0, concat_axis=0, tiled=True)  24.2 us
    dot_general x1, matrix products, per_device(): jnp.dot(normed, lax.all_gather(weight_flat, 'dp', axis=0, tiled=True), pr...  19.3 us
    another operation x3, other arithmetic  18.2 us
    all_to_all x1, starting transfers between devices, per_device(): lax.all_to_all(wanted, 'dp', split_axis=0, concat_axis=0, tiled=True)  13.1 us
    all_to_all x1, starting transfers between devices, per_device(): lax.all_to_all(looked, 'dp', split_axis=0, concat_axis=0, tiled=True)  11.7 us
  transfers between devices with their start and end apart: 5, of which 4 were waited for; matrix products, arithmetic and copies ran while one was open for 6% of the time, Pallas kernels for 0%

commit v1 on v0

--- a/solution.py
+++ b/solution.py
@@ -75,7 +75,9 @@
     weight_flat = user_weight.reshape(shard_rows, user_heads * triple)
     projected = jnp.dot(
         normed,
-        lax.all_gather(weight_flat, "dp", axis=0, tiled=True),
+        jnp.concatenate(
+            lax.all_to_all(jnp.stack([weight_flat] * lax.axis_size("dp")), "dp", 0, 0), axis=0
+        ),
         preferred_element_type=jnp.float32,
     )
     live = jnp.arange(length_seq, dtype=jnp.int32) < seq_length[0]

time: 403 us -> 506 us (1.26)
  waiting for transfers between devices: 265 us -> 357 us
  starting transfers between devices: 29.1 us -> 36.1 us
    all_to_all x0 -> x1, waiting for transfers between devices: none -> 176 us  [per_device(): lax.all_to_all(jnp.stack([weight_flat] * lax.axis_size('dp')), 'dp', 0, 0)]
    all_gather x1 -> x0, waiting for transfers between devices: 88.8 us -> none  [per_device(): lax.all_gather(weight_flat, 'dp', axis=0, tiled=True)]
    all_to_all x0 -> x1, starting transfers between devices: none -> 7.03 us  [per_device(): lax.all_to_all(jnp.stack([weight_flat] * lax.axis_size('dp')), 'dp', 0, 0)]
    another operation x2 -> x3, local copies, waits for them, and re-layouts: 0.09 us -> 6.08 us  [the longest x1 5.99 us: per_device(): jnp.stack([weight_flat] * lax.axis_size('dp'))]
where the time goes in v1:
time: 506 us; the launch traced here: 504 us
  waiting for transfers between devices  357 us (71%)
  local copies, waits for them, and re-layouts  37 us (7%)
  starting transfers between devices  36.1 us (7%)
  other arithmetic  32.7 us (6%)
  matrix products  26.8 us (5%)
  between operations  14.3 us (3%)
    all_to_all x1, waiting for transfers between devices, per_device(): lax.all_to_all(jnp.stack([weight_flat] * lax.axis_size('dp')), 'dp', 0, 0)  176 us
    all_gather x1, waiting for transfers between devices, per_device(): cited = lax.all_gather(cited, 'tp', axis=1, tiled=True)  84.1 us
    all_to_all x1, waiting for transfers between devices, per_device(): lax.all_to_all(looked, 'dp', split_axis=0, concat_axis=0, tiled=True)  72.4 us
    all_to_all x1, waiting for transfers between devices, sent_and_summed(): lax.all_to_all(parts, axis, split_axis=0, concat_axis=0, tiled=True)  24.2 us
    dot_general x1, matrix products, per_device(): jnp.dot(normed, jnp.concatenate(lax.all_to_all(jnp.stack([weight_flat] *...  19.4 us
    another operation x3, other arithmetic  18.2 us
    all_to_all x1, starting transfers between devices, per_device(): lax.all_to_all(wanted, 'dp', split_axis=0, concat_axis=0, tiled=True)  13.1 us
    all_to_all x1, starting transfers between devices, per_device(): lax.all_to_all(looked, 'dp', split_axis=0, concat_axis=0, tiled=True)  11.6 us
  transfers between devices with their start and end apart: 5, of which 4 were waited for; matrix products, arithmetic and copies ran while one was open for 6% of the time, Pallas kernels for 0%

profile of v1, /device:TPU:1, one launch (start us, length us, event | category | flops | bytes accessed | tf_op | source)
XLA Modules:
  0.0 503.5 jit_solution(18425990121933258665)
XLA Ops:
  6.5 0.8 fusion.23
  7.3 18.0 %reduce-window.6 = s32[64,8,128]{2,1,0:T(8,128)S(1)} reduce-window(s32[64,8,128]{2,1,0:T(8,128)S(1)} %fusion.23, s32[]{:T(128)} %constant.20.clone.1), window={size=1x1x128 pad=0_0x0_0x127_0}, to_apply=%region_0.0 | reduce-window | flops 8323072 | bytes 524292 | tf_op jit(solution)/shard_map/reduce-window
  25.9 0.8 fusion.22
  26.6 0.7 and_reduce_fusion
  27.4 4.5 scatter_custom_fusion
  31.8 0.7 all_to_all.15
  32.5 13.1 %all-to-all-start = ((s32[64,1,24]{2,1,0:T(1,128)}), s32[64,1,24]{2,1,0:T(1,128)S(1)}, u32[]{:S(2)}, u32[]{:S(2)}) async-start(s32[64,1,24]{2,1,0:T(1,128)} %bitcast.7), calls=%async_computation | async-start | bytes 65536 | tf_op jit(solution)/shard_map/all_to_all | solution.py:64
  45.7 1.3 reshape.154
  47.0 1.7 fusion.18
  48.9 0.2 copy.26
  49.1 0.7 fusion.16
  49.9 6.5 %copy.29 = bf16[4096,512]{1,0:T(8,128)(2,1)} copy(bf16[4096,512]{0,1:T(8,128)(2,1)} %bitcast.60) | data formatting | bytes 8388608 | tf_op jit(solution)/shard_map/dot_general | solution.py:45
  56.4 5.0 convolution_bitcast_fusion
  61.3 4.0 all-to-all-start.1
  65.4 0.6 broadcast.91
  66.0 0.8 reduce.7
  66.9 24.2 %all-to-all-done.1 = f32[4,128,1024]{2,1,0:T(8,128)S(1)} async-done(((f32[4,128,1024]{2,1,0:T(8,128)}), f32[4,128,1024]{2,1,0:T(8,128)S(1)}, u32[]{:S(2)}, u32[]{:S(2)}) %all-to-all-start.1) | async-done | bytes 2097184 | tf_op jit(solution)/shard_map/all_to_all | solution.py:17
  91.3 1.0 add_convert_fusion
  92.3 5.1 %gather_fusion = bf16[1536,1024]{1,0:T(8,128)(2,1)S(1)} fusion(bf16[128,1024]{1,0:T(8,128)(2,1)S(1)} %add_convert_fusion, s32[2048]{0:T(1024)S(1)} %pad_clamp_fusion), kind=kCustom, calls=%fused_computation | custom fusion | bytes 6297600 | tf_op jit(solution)/shard_map/jit(_take)/gather | solution.py:65
  97.4 1.9 broadcast_select_fusion
  99.3 11.6 %all-to-all-start.2 = ((bf16[64,24,1024]{2,1,0:T(8,128)(2,1)}), bf16[64,24,1024]{2,1,0:T(8,128)(2,1)S(1)}, u32[]{:S(2)}, u32[]{:S(2)}) async-start(bf16[64,24,1024]{2,1,0:T(8,128)(2,1)} %broadcast_select_fusion), calls=%async_computation.2 | async-start | bytes 6291456 | tf_op jit(solution)/shard_map/all_to_all | solution.py:68
  110.9 72.4 %all-to-all-done.2 = bf16[64,24,1024]{2,1,0:T(8,128)(2,1)S(1)} async-done(((bf16[64,24,1024]{2,1,0:T(8,128)(2,1)}), bf16[64,24,1024]{2,1,0:T(8,128)(2,1)S(1)}, u32[]{:S(2)}, u32[]{:S(2)}) %all-to-all-start.2) | async-done | bytes 3145760 | tf_op jit(solution)/shard_map/all_to_all | solution.py:68
  183.3 6.0 %stack.3 = bf16[64,64,1536]{2,1,0:T(8,128)(2,1)} broadcast(bf16[64,1536]{1,0:T(8,128)(2,1)S(1)} %bitcast.62), dimensions={1,2} | broadcast | bytes 12779520 | tf_op jit(solution)/shard_map/stack | solution.py:79
  189.3 7.0 %all-to-all-start.3 = ((bf16[64,64,1536]{2,1,0:T(8,128)(2,1)}), bf16[64,64,1536]{2,1,0:T(8,128)(2,1)}, u32[]{:S(2)}, u32[]{:S(2)}) async-start(bf16[64,64,1536]{2,1,0:T(8,128)(2,1)} %stack.3), calls=%async_computation.3 | async-start | bytes 25165824 | tf_op jit(solution)/shard_map/all_to_all | solution.py:79
  196.4 0.2 all-gather.2.cloned.1.call-start
  196.6 5.3 %gather_fusion.1 = bf16[1024,1024]{1,0:T(8,128)(2,1)} fusion(bf16[1536,1024]{1,0:T(8,128)(2,1)S(1)} %bitcast.57, s32[1024]{0:T(1024)S(1)} %broadcast_clamp_fusion), kind=kCustom, calls=%fused_computation.1 | custom fusion | bytes 4198400 | tf_op jit(solution)/shard_map/jit(_take)/gather | solution.py:69
  201.9 3.2 broadcast_select_fusion.1
  205.8 84.1 %all-gather.2.cloned.1.call-done = bf16[1024,4096]{1,0:T(8,128)(2,1)} async-done(((bf16[1024,1024]{1,0:T(8,128)(2,1)}), bf16[1024,4096]{1,0:T(8,128)(2,1)}) %all-gather.2.cloned.1.call-update) | async-done | bytes 8388624 | tf_op jit(solution)/shard_map/all_gather | solution.py:70
  289.9 5.1 %fusion.2 = f32[1024]{0:T(1024)S(1)} fusion(bf16[1024,4096]{1,0:T(8,128)(2,1)} %all-gather.2.cloned.1.call-done), kind=kLoop, calls=%fused_computation.7 | loop fusion | flops 12581888 | bytes 8392704 | tf_op jit(solution)/shard_map/reduce_sum | solution.py:72
  295.0 176.0 %all-to-all-done.3 = bf16[64,64,1536]{2,1,0:T(8,128)(2,1)} async-done(((bf16[64,64,1536]{2,1,0:T(8,128)(2,1)}), bf16[64,64,1536]{2,1,0:T(8,128)(2,1)}, u32[]{:S(2)}, u32[]{:S(2)}) %all-to-all-start.3) | async-done | bytes 12582944 | tf_op jit(solution)/shard_map/all_to_all | solution.py:79
  471.0 19.4 %select_convert_fusion = bf16[1024,1536]{1,0:T(8,128)(2,1)} fusion(bf16[4096,1536]{1,0:T(8,128)(2,1)} %bitcast.20, bf16[1024,4096]{1,0:T(8,128)(2,1)} %all-gather.2.cloned.1.call-done, f32[4096]{0:T(1024)S(1)} %copy-done.3, f32[1024]{0:T(1024)S(1)} %add_rsqrt_fusion, pred[1024]{0:T(1024)(128)(4,1)S(1)} %iota_compare_fusion.2), kind=kOutput, calls=%fused_computation.13 | convolution fusion | flops 12904824832 | bytes 24138752 | tf_op jit(solution)/shard_map/dot_general | solution.py:76
  490.4 6.2 %reshape.123 = bf16[1024,4,384]{2,1,0:T(4,128)(2,1)} reshape(bf16[1024,1536]{1,0:T(8,128)(2,1)} %select_convert_fusion) | data formatting | bytes 6291456 | tf_op jit(solution)/shard_map/reshape | solution.py:85
  (29 shorter events, 1.2 us)
Async XLA Ops:
  6.5 42.5 %copy-start = (bf16[128,4,512]{2,1,0:T(4,128)(2,1)S(1)}, bf16[128,4,512]{2,1,0:T(4,128)(2,1)}, u32[]{:S(2)}) copy-start(bf16[128,4,512]{2,1,0:T(4,128)(2,1)} %param.12) | copy-start | bytes 1572868
  32.5 28.8 %all-to-all-start = ((s32[64,1,24]{2,1,0:T(1,128)}), s32[64,1,24]{2,1,0:T(1,128)S(1)}, u32[]{:S(2)}, u32[]{:S(2)}) async-start(s32[64,1,24]{2,1,0:T(1,128)} %bitcast.7), calls=%async_computation | async-start | bytes 65536 | tf_op jit(solution)/shard_map/all_to_all | solution.py:64
  61.3 29.7 %all-to-all-start.1 = ((f32[4,128,1024]{2,1,0:T(8,128)}), f32[4,128,1024]{2,1,0:T(8,128)S(1)}, u32[]{:S(2)}, u32[]{:S(2)}) async-start(f32[4,128,1024]{2,1,0:T(8,128)} %convolution_bitcast_fusion), calls=%async_computation.1 | async-start | bytes 4194304 | tf_op jit(solution)/shard_map/all_to_all | solution.py:17
  99.3 11.6 %copy-start.2 = (bf16[64,4,384]{2,1,0:T(4,128)(2,1)S(1)}, bf16[64,4,384]{2,1,0:T(4,128)(2,1)}, u32[]{:S(2)}) copy-start(bf16[64,4,384]{2,1,0:T(4,128)(2,1)} %param.19) | copy-start | bytes 589828
  99.3 84.1 %all-to-all-start.2 = ((bf16[64,24,1024]{2,1,0:T(8,128)(2,1)}), bf16[64,24,1024]{2,1,0:T(8,128)(2,1)S(1)}, u32[]{:S(2)}, u32[]{:S(2)}) async-start(bf16[64,24,1024]{2,1,0:T(8,128)(2,1)} %broadcast_select_fusion), calls=%async_computation.2 | async-start | bytes 6291456 | tf_op jit(solution)/shard_map/all_to_all | solution.py:68
  189.3 281.6 %all-to-all-start.3 = ((bf16[64,64,1536]{2,1,0:T(8,128)(2,1)}), bf16[64,64,1536]{2,1,0:T(8,128)(2,1)}, u32[]{:S(2)}, u32[]{:S(2)}) async-start(bf16[64,64,1536]{2,1,0:T(8,128)(2,1)} %stack.3), calls=%async_computation.3 | async-start | bytes 25165824 | tf_op jit(solution)/shard_map/all_to_all | solution.py:79
  196.4 93.6 %all-gather.2.cloned.1.call-start = ((), (), s32[]{:S(2)}) async-start(), calls=%async_computation.4 | async-start | bytes 10485760 | tf_op jit(solution)/shard_map/all_gather | solution.py:70
  205.8 265.2 %copy-start.3 = (f32[4096]{0:T(1024)S(1)}, f32[4096]{0:T(1024)}, u32[]{:S(2)}) copy-start(f32[4096]{0:T(1024)} %param.18) | copy-start | bytes 49156
  471.0 25.7 %copy-start.1 = (bf16[128,4,512]{2,1,0:T(4,128)(2,1)S(1)}, bf16[128,4,512]{2,1,0:T(4,128)(2,1)}, u32[]{:S(2)}) copy-start(bf16[128,4,512]{2,1,0:T(4,128)(2,1)} %param.12) | copy-start | bytes 1572868
Sparse Core Ops, SparseCore 0:
  205.3 84.6 all-gather.1
